TPU v7x, 32 devices: a whole 2x2x4 slice. The times are simulated.
32 devices in a mesh: lang: 2 (over y), clu: 16 (over z, x, core).
Axes of the slice: x: 2, y: 2, z: 4, core: 2. Of those that a mesh axis runs over, the one named last changes fastest.
Arguments:
- embeddings: bfloat16 [8192, 1024], P(('lang', 'clu')), parts along dimension 0, may hold values from -6 to 6
- assignment: int32 [8192, 1], P(('lang', 'clu')), parts along dimension 0, may hold values from 0 to 31; in each aligned block of 256 rows (0 to 255, 256 to 511, ...) at most 16 rows name the same one
Outputs:
- best_similarity: float32 [8192], P(('lang', 'clu')), parts along dimension 0
There are 2 independent parts, one for each index of `lang`. A program takes and returns all parts, laid end to end along the dimension named above; each array names one. Nothing has to cross between parts.
Inputs may be any that keep to these rules, and one draw needn't show every extreme that they name: `assignment`: in each aligned block of 256 rows (the rows of one device) no cluster is named by more than 16 rows; every cluster is named by some row.
All inputs are finite; a program needn't handle non-finite values.
Results may differ from a plain program's by a relative error of at most 0.0016.
Values may be sent and summed in bfloat16 or wider, within the bound.
No kernel may reach another device: no remote copies, remote signals or barrier semaphores. Data moves between devices by JAX's collectives and lax.ppermute only.
A program may use at most 64 MiB of HBM per device.

v0:
```python
import jax
import jax.numpy as jnp
from jax import lax
from jax.sharding import PartitionSpec as P

CLU_DEV = 2
EPS = 1e-06


def normalize(embeddings):
    values = embeddings.astype(jnp.float32)
    scale = lax.rsqrt(jnp.sum(values * values, axis=-1, keepdims=True) + EPS)
    return (values * scale).astype(jnp.bfloat16)


def slot_index(cluster, groups, most):
    count = cluster.shape[0]
    order = jnp.argsort(cluster, stable=True)
    ranked = cluster[order]
    first = jnp.searchsorted(ranked, ranked, side="left")
    rank_sorted = jnp.arange(count, dtype=jnp.int32) - first
    rank = jnp.zeros((count,), jnp.int32).at[order].set(rank_sorted)
    local = cluster % CLU_DEV
    owner = cluster // CLU_DEV
    return (local * groups + owner) * most + rank


def cluster_scores(pieces):
    rows, flags = pieces
    items = rows.shape[0]
    width = rows.shape[1] * rows.shape[2]
    rows = rows.reshape(items, width, rows.shape[3])
    flags = flags.reshape(items, width)
    offsets = jnp.arange(width, dtype=jnp.int32)
    distinct = offsets[:, None] != offsets[None, :]

    def single(pair):
        block, marks = pair
        gram = lax.dot_general(
            block, block, (((1,), (1,)), ((), ())), preferred_element_type=jnp.float32
        )
        keep = distinct & (marks > 0)[None, :]
        best = jnp.max(jnp.where(keep, gram, jnp.float32(-2.0)), axis=1)
        return jnp.maximum(best, jnp.float32(-1.0))

    best = lax.map(single, (rows, flags))
    return best.reshape(items, 1, width)


def shards(embeddings, assignment):
    groups = lax.axis_size("clu")
    count = embeddings.shape[0]
    width = embeddings.shape[1]
    most = 2 * count // (CLU_DEV * groups)
    unit = normalize(embeddings)
    cluster = assignment[:, 0]
    slot = slot_index(cluster, groups, most)
    total = CLU_DEV * groups * most
    outgoing = jnp.zeros((total, width), jnp.bfloat16).at[slot].set(unit)
    marks = jnp.zeros((total,), jnp.bfloat16).at[slot].set(jnp.ones((count,), jnp.bfloat16))
    outgoing = outgoing.reshape(CLU_DEV, groups, most, width)
    marks = marks.reshape(CLU_DEV, groups, most)
    arrived = (
        lax.all_to_all(outgoing, "clu", split_axis=1, concat_axis=2, tiled=True),
        lax.all_to_all(marks, "clu", split_axis=1, concat_axis=2, tiled=True),
    )
    best = cluster_scores(arrived)
    returned = lax.all_to_all(best, "clu", split_axis=2, concat_axis=1, tiled=True)
    return returned.reshape(total)[slot]


def solution(mesh):
    in_specs = (P(("lang", "clu"), None), P(("lang", "clu"), None))
    out_specs = P(("lang", "clu"))
    return jax.shard_map(shards, mesh=mesh, in_specs=in_specs, out_specs=out_specs, check_vma=False)
```

profile of v0, /device:TPU:0, one launch (start us, length us, event | category | flops | bytes accessed | tf_op | source)
XLA Modules:
  0.0 87.9 jit_solution(13854131566071930487)
XLA Ops:
  0.0 0.0 copy-start
  0.0 0.7 copy-done
  0.7 3.2 %sort.17 = (s32[256]{0:T(256)}, s32[256]{0:T(256)S(1)}) sort(s32[256]{0:T(256)S(1)} %bitcast.15, s32[256]{0:T(256)S(1)} %iota.14), dimensions={0}, to_apply=%region_0.0 | sort | flops 2048 | bytes 4096 | tf_op jit(solution)/shard_map/jit(argsort)/sort | solution.py:18
  3.9 1.9 %gather_fusion.1 = s32[256]{0:T(256)S(1)} fusion(s32[256]{0:T(256)S(1)} %bitcast.16, s32[1024]{0:T(1024)S(1)} %pad_clamp_fusion.2), kind=kCustom, calls=%fused_computation.1 | custom fusion | bytes 3072 | tf_op jit(solution)/shard_map/gather | solution.py:19
  5.8 0.0 copy-start.1
  5.8 18.4 %while.37 = (s32[]{:T(128)}, u32[256]{0:T(256)S(1)}, u32[256]{0:T(256)S(1)}, s32[256]{0:T(256)S(1)}, s32[]{:T(128)}, /*index=5*/s32[]{:T(128)}, s32[]{}) while((s32[]{:T(128)}, u32[256]{0:T(256)S(1)}, u32[256]{0:T(256)S(1)}, s32[256]{0:T(256)S(1)}, s32[]{:T(128)}, /*index=5*/s32[]{:T(128)}, s32[]{}) %tuple.52), condition=%wide.region_2.3_spmd.clone, body=%wide.region_1.0_spmd.clone.sunk | while | flops 5636 | bytes 22117 | solution.py:20
  5.9 1.9 %gather_fusion = s32[256]{0:T(256)S(1)} fusion(s32[256]{0:T(256)S(1)} %get-tuple-element.217, u32[1024]{0:T(1024)S(1)} %pad_clamp_fusion.4), kind=kCustom, calls=%fused_computation.clone.clone.1 | custom fusion | bytes 3072 | tf_op jit(solution)/shard_map/jit(searchsorted)/jit(_searchsorted_scan_impl)/vmap(jit(_searchsorted_scan_impl))/while/body/eval_jaxpr/gather | solution.py:20
  7.9 1.9 %gather_fusion = s32[256]{0:T(256)S(1)} fusion(s32[256]{0:T(256)S(1)} %get-tuple-element.217, u32[1024]{0:T(1024)S(1)} %pad_clamp_fusion.4), kind=kCustom, calls=%fused_computation.clone.clone.1 | custom fusion | bytes 3072 | tf_op jit(solution)/shard_map/jit(searchsorted)/jit(_searchsorted_scan_impl)/vmap(jit(_searchsorted_scan_impl))/while/body/eval_jaxpr/gather | solution.py:20
  9.9 1.9 %gather_fusion = s32[256]{0:T(256)S(1)} fusion(s32[256]{0:T(256)S(1)} %get-tuple-element.217, u32[1024]{0:T(1024)S(1)} %pad_clamp_fusion.4), kind=kCustom, calls=%fused_computation.clone.clone.1 | custom fusion | bytes 3072 | tf_op jit(solution)/shard_map/jit(searchsorted)/jit(_searchsorted_scan_impl)/vmap(jit(_searchsorted_scan_impl))/while/body/eval_jaxpr/gather | solution.py:20
  12.0 1.9 %gather_fusion = s32[256]{0:T(256)S(1)} fusion(s32[256]{0:T(256)S(1)} %get-tuple-element.217, u32[1024]{0:T(1024)S(1)} %pad_clamp_fusion.4), kind=kCustom, calls=%fused_computation.clone.clone.1 | custom fusion | bytes 3072 | tf_op jit(solution)/shard_map/jit(searchsorted)/jit(_searchsorted_scan_impl)/vmap(jit(_searchsorted_scan_impl))/while/body/eval_jaxpr/gather | solution.py:20
  14.0 1.9 %gather_fusion = s32[256]{0:T(256)S(1)} fusion(s32[256]{0:T(256)S(1)} %get-tuple-element.217, u32[1024]{0:T(1024)S(1)} %pad_clamp_fusion.4), kind=kCustom, calls=%fused_computation.clone.clone.1 | custom fusion | bytes 3072 | tf_op jit(solution)/shard_map/jit(searchsorted)/jit(_searchsorted_scan_impl)/vmap(jit(_searchsorted_scan_impl))/while/body/eval_jaxpr/gather | solution.py:20
  16.1 1.9 %gather_fusion = s32[256]{0:T(256)S(1)} fusion(s32[256]{0:T(256)S(1)} %get-tuple-element.217, u32[1024]{0:T(1024)S(1)} %pad_clamp_fusion.4), kind=kCustom, calls=%fused_computation.clone.clone.1 | custom fusion | bytes 3072 | tf_op jit(solution)/shard_map/jit(searchsorted)/jit(_searchsorted_scan_impl)/vmap(jit(_searchsorted_scan_impl))/while/body/eval_jaxpr/gather | solution.py:20
  18.1 1.9 %gather_fusion = s32[256]{0:T(256)S(1)} fusion(s32[256]{0:T(256)S(1)} %get-tuple-element.217, u32[1024]{0:T(1024)S(1)} %pad_clamp_fusion.4), kind=kCustom, calls=%fused_computation.clone.clone.1 | custom fusion | bytes 3072 | tf_op jit(solution)/shard_map/jit(searchsorted)/jit(_searchsorted_scan_impl)/vmap(jit(_searchsorted_scan_impl))/while/body/eval_jaxpr/gather | solution.py:20
  20.1 1.9 %gather_fusion = s32[256]{0:T(256)S(1)} fusion(s32[256]{0:T(256)S(1)} %get-tuple-element.217, u32[1024]{0:T(1024)S(1)} %pad_clamp_fusion.4), kind=kCustom, calls=%fused_computation.clone.clone.1 | custom fusion | bytes 3072 | tf_op jit(solution)/shard_map/jit(searchsorted)/jit(_searchsorted_scan_impl)/vmap(jit(_searchsorted_scan_impl))/while/body/eval_jaxpr/gather | solution.py:20
  22.2 1.9 %gather_fusion = s32[256]{0:T(256)S(1)} fusion(s32[256]{0:T(256)S(1)} %get-tuple-element.217, u32[1024]{0:T(1024)S(1)} %pad_clamp_fusion.4), kind=kCustom, calls=%fused_computation.clone.clone.1 | custom fusion | bytes 3072 | tf_op jit(solution)/shard_map/jit(searchsorted)/jit(_searchsorted_scan_impl)/vmap(jit(_searchsorted_scan_impl))/while/body/eval_jaxpr/gather | solution.py:20
  24.2 1.4 %scatter_custom_fusion = s32[256]{0:T(256)S(1)} fusion(s32[256]{0:T(256)S(1)} %compare_select_fusion.1, s32[256]{0:T(256)S(1)} %convert_subtract_fusion, s32[]{:T(128)} %constant.83.clone.1), kind=kCustom, calls=%fused_computation.42 | custom fusion | bytes 1028 | tf_op jit(solution)/shard_map/scatter | solution.py:22
  25.6 2.2 %scatter_custom_fusion.1 = bf16[512]{0:T(512)(128)(2,1)S(1)} fusion(s32[256]{0:T(256)S(1)} %compare_select_fusion, bf16[256]{0:T(256)(128)(2,1)S(1)} %broadcast.47, bf16[]{:T(256)} %constant.85.clone.1), kind=kCustom, calls=%fused_computation.44 | custom fusion | bytes 1026 | tf_op jit(solution)/shard_map/scatter | solution.py:60
  27.8 0.1 reshape.45
  27.9 0.6 copy.5
  28.5 7.4 %all-to-all-start = ((bf16[2,16,16]{2,0,1:T(2,128)(2,1)}), bf16[2,16,16]{2,0,1:T(2,128)(2,1)S(1)}, u32[]{:S(2)}, u32[]{:S(2)}) async-start(bf16[2,16,16]{2,0,1:T(2,128)(2,1)} %copy.5), calls=%async_computation | async-start | bytes 16384 | tf_op jit(solution)/shard_map/all_to_all | solution.py:65
  35.9 0.0 copy-done.1
  35.9 0.2 fusion.9
  36.1 2.0 %scatter_custom_fusion.2 = bf16[512,1024]{1,0:T(8,128)(2,1)S(1)} fusion(s32[256]{0:T(256)S(1)} %compare_select_fusion, bf16[256,1024]{1,0:T(8,128)(2,1)S(1)} %copy-done.1, f32[256]{0:T(256)S(1)} %add_rsqrt_fusion, bf16[]{:T(256)} %constant.85.clone.1), kind=kCustom, calls=%fused_computation.26 | custom fusion | flops 786432 | bytes 1573890 | tf_op jit(solution)/shard_map/scatter | solution.py:59
  38.1 1.1 %copy.7 = bf16[2,16,16,1024]{3,2,0,1:T(8,128)(2,1)} copy(bf16[2,16,16,1024]{3,2,1,0:T(8,128)(2,1)S(1)} %bitcast.19) | data formatting | bytes 2097152 | tf_op jit(solution)/shard_map/reshape | solution.py:61
  39.2 3.2 %all-to-all-done = bf16[2,16,16]{2,0,1:T(2,128)(2,1)S(1)} async-done(((bf16[2,16,16]{2,0,1:T(2,128)(2,1)}), bf16[2,16,16]{2,0,1:T(2,128)(2,1)S(1)}, u32[]{:S(2)}, u32[]{:S(2)}) %all-to-all-start) | async-done | bytes 1056 | tf_op jit(solution)/shard_map/all_to_all | solution.py:65
  42.3 3.7 %all-to-all-start.1 = ((bf16[2,16,16,1024]{3,2,0,1:T(8,128)(2,1)}), bf16[2,16,16,1024]{3,2,0,1:T(8,128)(2,1)S(1)}, u32[]{:S(2)}, u32[]{:S(2)}) async-start(bf16[2,16,16,1024]{3,2,0,1:T(8,128)(2,1)} %copy.7), calls=%async_computation.1 | async-start | bytes 2097152 | tf_op jit(solution)/shard_map/all_to_all | solution.py:64
  46.0 0.1 reshape.46
  46.1 22.7 %all-to-all-done.1 = bf16[2,16,16,1024]{3,2,0,1:T(8,128)(2,1)S(1)} async-done(((bf16[2,16,16,1024]{3,2,0,1:T(8,128)(2,1)}), bf16[2,16,16,1024]{3,2,0,1:T(8,128)(2,1)S(1)}, u32[]{:S(2)}, u32[]{:S(2)}) %all-to-all-start.1) | async-done | bytes 1048608 | tf_op jit(solution)/shard_map/all_to_all | solution.py:64
  68.8 0.1 copy.8
  68.9 0.9 %while.36 = (s32[]{:T(128)}, f32[2,256]{1,0:T(2,128)S(1)}, bf16[2,256]{1,0:T(2,128)(2,1)S(1)}, bf16[2,256,1024]{2,1,0:T(8,128)(2,1)S(1)}, s32[]{:T(128)}, /*index=5*/s32[]{:T(128)}) while((s32[]{:T(128)}, f32[2,256]{1,0:T(2,128)S(1)}, bf16[2,256]{1,0:T(2,128)(2,1)S(1)}, bf16[2,256,1024]{2,1,0:T(8,128)(2,1)S(1)}, s32[]{:T(128)}, ...), condition=%wide.region_9.10_spmd.clone, body=%wide.region_7.9_spmd.clone.sunk | while | flops 134480640 | bytes 530769 | solution.py:46
  69.0 0.4 fusion.26
  69.4 0.4 fusion.26
  69.8 0.8 copy.9
  70.6 6.7 %all-to-all-start.2 = ((f32[2,1,256]{0,1,2:T(1,128)}), f32[2,1,256]{0,1,2:T(1,128)S(1)}, u32[]{:S(2)}, u32[]{:S(2)}) async-start(f32[2,1,256]{0,1,2:T(1,128)} %bitcast.3), calls=%async_computation.2 | async-start | bytes 262144 | tf_op jit(solution)/shard_map/all_to_all | solution.py:68
  77.4 7.9 %all-to-all-done.2 = f32[2,1,256]{0,1,2:T(1,128)S(1)} async-done(((f32[2,1,256]{0,1,2:T(1,128)}), f32[2,1,256]{0,1,2:T(1,128)S(1)}, u32[]{:S(2)}, u32[]{:S(2)}) %all-to-all-start.2) | async-done | bytes 2080 | tf_op jit(solution)/shard_map/all_to_all | solution.py:68
  85.3 0.1 copy.10
  85.4 2.5 %gather_fusion.2 = f32[256]{0:T(256)} fusion(f32[512]{0:T(512)S(1)} %bitcast.18, s32[1024]{0:T(1024)S(1)} %pad_clamp_fusion.1), kind=kCustom, calls=%fused_computation.2 | custom fusion | bytes 3072 | tf_op jit(solution)/shard_map/gather | solution.py:69
  (64 shorter events, 0.6 us)
Async XLA Ops:
  0.0 0.7 copy-start
  5.8 30.1 %copy-start.1 = (bf16[256,1024]{1,0:T(8,128)(2,1)S(1)}, bf16[256,1024]{1,0:T(8,128)(2,1)}, u32[]{:S(2)}) copy-start(bf16[256,1024]{1,0:T(8,128)(2,1)} %param.6) | copy-start | bytes 1572868
  28.5 13.8 %all-to-all-start = ((bf16[2,16,16]{2,0,1:T(2,128)(2,1)}), bf16[2,16,16]{2,0,1:T(2,128)(2,1)S(1)}, u32[]{:S(2)}, u32[]{:S(2)}) async-start(bf16[2,16,16]{2,0,1:T(2,128)(2,1)} %copy.5), calls=%async_computation | async-start | bytes 16384 | tf_op jit(solution)/shard_map/all_to_all | solution.py:65
  42.3 26.5 %all-to-all-start.1 = ((bf16[2,16,16,1024]{3,2,0,1:T(8,128)(2,1)}), bf16[2,16,16,1024]{3,2,0,1:T(8,128)(2,1)S(1)}, u32[]{:S(2)}, u32[]{:S(2)}) async-start(bf16[2,16,16,1024]{3,2,0,1:T(8,128)(2,1)} %copy.7), calls=%async_computation.1 | async-start | bytes 2097152 | tf_op jit(solution)/shard_map/all_to_all | solution.py:64
  70.6 14.6 %all-to-all-start.2 = ((f32[2,1,256]{0,1,2:T(1,128)}), f32[2,1,256]{0,1,2:T(1,128)S(1)}, u32[]{:S(2)}, u32[]{:S(2)}) async-start(f32[2,1,256]{0,1,2:T(1,128)} %bitcast.3), calls=%async_computation.2 | async-start | bytes 262144 | tf_op jit(solution)/shard_map/all_to_all | solution.py:68
where the time goes:
time: 88.2 us; the launch traced here: 87.9 us
  waiting for transfers between devices  33.8 us (38%)
  local copies, waits for them, and re-layouts  29.1 us (33%)
  starting transfers between devices  17.8 us (20%)
  other arithmetic  5.78 us (7%)
    all_to_all x1, waiting for transfers between devices, shards(): lax.all_to_all(outgoing, 'clu', split_axis=1, concat_axis=2, tiled=True)  22.7 us
    gather x9, local copies, waits for them, and re-layouts, slot_index(): first = jnp.searchsorted(ranked, ranked, side='left')  17.5 us
    all_to_all x1, waiting for transfers between devices, shards(): lax.all_to_all(best, 'clu', split_axis=2, concat_axis=1, tiled=True)  7.89 us
    all_to_all x1, starting transfers between devices, shards(): lax.all_to_all(marks, 'clu', split_axis=1, concat_axis=2, tiled=True)  7.39 us
    all_to_all x1, starting transfers between devices, shards(): lax.all_to_all(best, 'clu', split_axis=2, concat_axis=1, tiled=True)  6.74 us
    all_to_all x1, starting transfers between devices, shards(): lax.all_to_all(outgoing, 'clu', split_axis=1, concat_axis=2, tiled=True)  3.65 us
    all_to_all x1, waiting for transfers between devices, shards(): lax.all_to_all(marks, 'clu', split_axis=1, concat_axis=2, tiled=True)  3.18 us
    sort x1, other arithmetic, slot_index(): order = jnp.argsort(cluster, stable=True)  3.16 us
  transfers between devices with their start and end apart: 3, of which 3 were waited for; matrix products, arithmetic and copies ran while one was open for 4% of the time, Pallas kernels for 0%

commit v1 on v0

--- a/solution.py
+++ b/solution.py
@@ -65,7 +65,19 @@
         lax.all_to_all(marks, "clu", split_axis=1, concat_axis=2, tiled=True),
     )
     best = cluster_scores(arrived)
-    returned = lax.all_to_all(best, "clu", split_axis=2, concat_axis=1, tiled=True)
+    ways, here = (lax.axis_size("clu"), lax.axis_index("clu"))
+    width_2 = best.shape[2] // ways
+    shape = list(best.shape)
+    shape[2] = width_2
+    height = shape[1]
+    shape[1] = height * ways
+    full = jnp.zeros(shape, best.dtype)
+    for mask in range(ways):
+        part = lax.dynamic_slice_in_dim(best, (here ^ mask) * width_2, width_2, axis=2)
+        if mask:
+            part = lax.ppermute(part, "clu", [(d, d ^ mask) for d in range(ways)])
+        full = lax.dynamic_update_slice_in_dim(full, part, (here ^ mask) * height, axis=1)
+    returned = full
     return returned.reshape(total)[slot]
 
 

time: 88.2 us -> 101 us (1.15)
  starting transfers between devices: 17.8 us -> 34.3 us
  waiting for transfers between devices: 33.8 us -> 30.2 us
    ppermute x0 -> x15, starting transfers between devices: none -> 23.2 us  [shards(): part = lax.ppermute(part, 'clu', [(d, d ^ mask) for d in range(ways)])]
    all_to_all x1 -> x0, waiting for transfers between devices: 7.89 us -> none  [shards(): lax.all_to_all(best, 'clu', split_axis=2, concat_axis=1, tiled=True)]
    all_to_all x1 -> x0, starting transfers between devices: 6.74 us -> none  [shards(): lax.all_to_all(best, 'clu', split_axis=2, concat_axis=1, tiled=True)]
    ppermute x0 -> x15, waiting for transfers between devices: none -> 4.57 us  [shards(): part = lax.ppermute(part, 'clu', [(d, d ^ mask) for d in range(ways)])]
  transfers between devices with their start and end apart: 3 -> 17, of which waited for: 3 -> 4; matrix products, arithmetic and copies ran while one was open for 4% -> 4% of each run, Pallas kernels for 0% -> 0%
where the time goes in v1:
time: 101 us
  starting transfers between devices  34.3 us (34%)
  waiting for transfers between devices  30.2 us (30%)
  local copies, waits for them, and re-layouts  28.9 us (29%)
  other arithmetic  5.78 us (6%)
    ppermute x15, starting transfers between devices, shards(): part = lax.ppermute(part, 'clu', [(d, d ^ mask) for d in range(ways)])  23.2 us
    all_to_all x1, waiting for transfers between devices, shards(): lax.all_to_all(outgoing, 'clu', split_axis=1, concat_axis=2, tiled=True)  22.4 us
    gather x9, local copies, waits for them, and re-layouts, slot_index(): first = jnp.searchsorted(ranked, ranked, side='left')  17.5 us
    all_to_all x1, starting transfers between devices, shards(): lax.all_to_all(marks, 'clu', split_axis=1, concat_axis=2, tiled=True)  7.39 us
    ppermute x15, waiting for transfers between devices, shards(): part = lax.ppermute(part, 'clu', [(d, d ^ mask) for d in range(ways)])  4.57 us
    all_to_all x1, starting transfers between devices, shards(): lax.all_to_all(outgoing, 'clu', split_axis=1, concat_axis=2, tiled=True)  3.65 us
    all_to_all x1, waiting for transfers between devices, shards(): lax.all_to_all(marks, 'clu', split_axis=1, concat_axis=2, tiled=True)  3.2 us
    sort x1, other arithmetic, slot_index(): order = jnp.argsort(cluster, stable=True)  3.16 us
  transfers between devices with their start and end apart: 17, of which 4 were waited for; matrix products, arithmetic and copies ran while one was open for 4% of the time, Pallas kernels for 0%

profile of v1, /device:TPU:0, one launch (start us, length us, event | category | flops | bytes accessed | tf_op | source)
XLA Modules:
  0.0 100.9 jit_solution(7162420280068988856)
XLA Ops:
  0.0 0.7 copy-done
  0.7 3.2 %sort.17 = (s32[256]{0:T(256)}, s32[256]{0:T(256)S(1)}) sort(s32[256]{0:T(256)S(1)} %bitcast.59, s32[256]{0:T(256)S(1)} %iota.14), dimensions={0}, to_apply=%region_0.0 | sort | flops 2048 | bytes 4096 | tf_op jit(solution)/shard_map/jit(argsort)/sort | solution.py:18
  3.9 1.9 %gather_fusion.1 = s32[256]{0:T(256)S(1)} fusion(s32[256]{0:T(256)S(1)} %bitcast.60, s32[1024]{0:T(1024)S(1)} %pad_clamp_fusion.2), kind=kCustom, calls=%fused_computation.1 | custom fusion | bytes 3072 | tf_op jit(solution)/shard_map/gather | solution.py:19
  5.8 18.4 %while.37 = (s32[]{:T(128)}, u32[256]{0:T(256)S(1)}, u32[256]{0:T(256)S(1)}, s32[256]{0:T(256)S(1)}, s32[]{:T(128)}, /*index=5*/s32[]{:T(128)}, s32[]{}) while((s32[]{:T(128)}, u32[256]{0:T(256)S(1)}, u32[256]{0:T(256)S(1)}, s32[256]{0:T(256)S(1)}, s32[]{:T(128)}, /*index=5*/s32[]{:T(128)}, s32[]{}) %tuple.67), condition=%wide.region_2.3_spmd.clone, body=%wide.region_1.0_spmd.clone.sunk | while | flops 5636 | bytes 22117 | solution.py:20
  5.9 1.9 %gather_fusion = s32[256]{0:T(256)S(1)} fusion(s32[256]{0:T(256)S(1)} %get-tuple-element.233, u32[1024]{0:T(1024)S(1)} %pad_clamp_fusion.4), kind=kCustom, calls=%fused_computation.clone.clone.1 | custom fusion | bytes 3072 | tf_op jit(solution)/shard_map/jit(searchsorted)/jit(_searchsorted_scan_impl)/vmap(jit(_searchsorted_scan_impl))/while/body/eval_jaxpr/gather | solution.py:20
  7.9 1.9 %gather_fusion = s32[256]{0:T(256)S(1)} fusion(s32[256]{0:T(256)S(1)} %get-tuple-element.233, u32[1024]{0:T(1024)S(1)} %pad_clamp_fusion.4), kind=kCustom, calls=%fused_computation.clone.clone.1 | custom fusion | bytes 3072 | tf_op jit(solution)/shard_map/jit(searchsorted)/jit(_searchsorted_scan_impl)/vmap(jit(_searchsorted_scan_impl))/while/body/eval_jaxpr/gather | solution.py:20
  9.9 1.9 %gather_fusion = s32[256]{0:T(256)S(1)} fusion(s32[256]{0:T(256)S(1)} %get-tuple-element.233, u32[1024]{0:T(1024)S(1)} %pad_clamp_fusion.4), kind=kCustom, calls=%fused_computation.clone.clone.1 | custom fusion | bytes 3072 | tf_op jit(solution)/shard_map/jit(searchsorted)/jit(_searchsorted_scan_impl)/vmap(jit(_searchsorted_scan_impl))/while/body/eval_jaxpr/gather | solution.py:20
  12.0 1.9 %gather_fusion = s32[256]{0:T(256)S(1)} fusion(s32[256]{0:T(256)S(1)} %get-tuple-element.233, u32[1024]{0:T(1024)S(1)} %pad_clamp_fusion.4), kind=kCustom, calls=%fused_computation.clone.clone.1 | custom fusion | bytes 3072 | tf_op jit(solution)/shard_map/jit(searchsorted)/jit(_searchsorted_scan_impl)/vmap(jit(_searchsorted_scan_impl))/while/body/eval_jaxpr/gather | solution.py:20
  14.0 1.9 %gather_fusion = s32[256]{0:T(256)S(1)} fusion(s32[256]{0:T(256)S(1)} %get-tuple-element.233, u32[1024]{0:T(1024)S(1)} %pad_clamp_fusion.4), kind=kCustom, calls=%fused_computation.clone.clone.1 | custom fusion | bytes 3072 | tf_op jit(solution)/shard_map/jit(searchsorted)/jit(_searchsorted_scan_impl)/vmap(jit(_searchsorted_scan_impl))/while/body/eval_jaxpr/gather | solution.py:20
  16.1 1.9 %gather_fusion = s32[256]{0:T(256)S(1)} fusion(s32[256]{0:T(256)S(1)} %get-tuple-element.233, u32[1024]{0:T(1024)S(1)} %pad_clamp_fusion.4), kind=kCustom, calls=%fused_computation.clone.clone.1 | custom fusion | bytes 3072 | tf_op jit(solution)/shard_map/jit(searchsorted)/jit(_searchsorted_scan_impl)/vmap(jit(_searchsorted_scan_impl))/while/body/eval_jaxpr/gather | solution.py:20
  18.1 1.9 %gather_fusion = s32[256]{0:T(256)S(1)} fusion(s32[256]{0:T(256)S(1)} %get-tuple-element.233, u32[1024]{0:T(1024)S(1)} %pad_clamp_fusion.4), kind=kCustom, calls=%fused_computation.clone.clone.1 | custom fusion | bytes 3072 | tf_op jit(solution)/shard_map/jit(searchsorted)/jit(_searchsorted_scan_impl)/vmap(jit(_searchsorted_scan_impl))/while/body/eval_jaxpr/gather | solution.py:20
  20.1 1.9 %gather_fusion = s32[256]{0:T(256)S(1)} fusion(s32[256]{0:T(256)S(1)} %get-tuple-element.233, u32[1024]{0:T(1024)S(1)} %pad_clamp_fusion.4), kind=kCustom, calls=%fused_computation.clone.clone.1 | custom fusion | bytes 3072 | tf_op jit(solution)/shard_map/jit(searchsorted)/jit(_searchsorted_scan_impl)/vmap(jit(_searchsorted_scan_impl))/while/body/eval_jaxpr/gather | solution.py:20
  22.2 1.9 %gather_fusion = s32[256]{0:T(256)S(1)} fusion(s32[256]{0:T(256)S(1)} %get-tuple-element.233, u32[1024]{0:T(1024)S(1)} %pad_clamp_fusion.4), kind=kCustom, calls=%fused_computation.clone.clone.1 | custom fusion | bytes 3072 | tf_op jit(solution)/shard_map/jit(searchsorted)/jit(_searchsorted_scan_impl)/vmap(jit(_searchsorted_scan_impl))/while/body/eval_jaxpr/gather | solution.py:20
  24.2 1.4 %scatter_custom_fusion = s32[256]{0:T(256)S(1)} fusion(s32[256]{0:T(256)S(1)} %compare_select_fusion.1, s32[256]{0:T(256)S(1)} %convert_subtract_fusion, s32[]{:T(128)} %constant.104.clone.1), kind=kCustom, calls=%fused_computation.73 | custom fusion | bytes 1028 | tf_op jit(solution)/shard_map/scatter | solution.py:22
  25.6 2.2 %scatter_custom_fusion.1 = bf16[512]{0:T(512)(128)(2,1)S(1)} fusion(s32[256]{0:T(256)S(1)} %compare_select_fusion, bf16[256]{0:T(256)(128)(2,1)S(1)} %broadcast.50, bf16[]{:T(256)} %constant.105.clone.1), kind=kCustom, calls=%fused_computation.75 | custom fusion | bytes 1026 | tf_op jit(solution)/shard_map/scatter | solution.py:60
  27.8 0.1 reshape.55
  27.9 0.6 copy.36
  28.5 7.4 %all-to-all-start = ((bf16[2,16,16]{2,0,1:T(2,128)(2,1)}), bf16[2,16,16]{2,0,1:T(2,128)(2,1)S(1)}, u32[]{:S(2)}, u32[]{:S(2)}) async-start(bf16[2,16,16]{2,0,1:T(2,128)(2,1)} %copy.36), calls=%async_computation | async-start | bytes 16384 | tf_op jit(solution)/shard_map/all_to_all | solution.py:65
  35.9 0.2 fusion.9
  36.1 2.0 %scatter_custom_fusion.2 = bf16[512,1024]{1,0:T(8,128)(2,1)S(1)} fusion(s32[256]{0:T(256)S(1)} %compare_select_fusion, bf16[256,1024]{1,0:T(8,128)(2,1)S(1)} %copy-done.1, f32[256]{0:T(256)S(1)} %add_rsqrt_fusion, bf16[]{:T(256)} %constant.105.clone.1), kind=kCustom, calls=%fused_computation.26 | custom fusion | flops 786432 | bytes 1573890 | tf_op jit(solution)/shard_map/scatter | solution.py:59
  38.1 1.0 %copy.38 = bf16[2,16,16,1024]{3,2,0,1:T(8,128)(2,1)} copy(bf16[2,16,16,1024]{3,2,1,0:T(8,128)(2,1)S(1)} %bitcast.62) | data formatting | bytes 2097152 | tf_op jit(solution)/shard_map/reshape | solution.py:61
  39.1 3.2 %all-to-all-done = bf16[2,16,16]{2,0,1:T(2,128)(2,1)S(1)} async-done(((bf16[2,16,16]{2,0,1:T(2,128)(2,1)}), bf16[2,16,16]{2,0,1:T(2,128)(2,1)S(1)}, u32[]{:S(2)}, u32[]{:S(2)}) %all-to-all-start) | async-done | bytes 1056 | tf_op jit(solution)/shard_map/all_to_all | solution.py:65
  42.3 3.7 %all-to-all-start.1 = ((bf16[2,16,16,1024]{3,2,0,1:T(8,128)(2,1)}), bf16[2,16,16,1024]{3,2,0,1:T(8,128)(2,1)S(1)}, u32[]{:S(2)}, u32[]{:S(2)}) async-start(bf16[2,16,16,1024]{3,2,0,1:T(8,128)(2,1)} %copy.38), calls=%async_computation.1 | async-start | bytes 2097152 | tf_op jit(solution)/shard_map/all_to_all | solution.py:64
  46.3 0.1 reshape.56
  46.4 22.4 %all-to-all-done.1 = bf16[2,16,16,1024]{3,2,0,1:T(8,128)(2,1)S(1)} async-done(((bf16[2,16,16,1024]{3,2,0,1:T(8,128)(2,1)}), bf16[2,16,16,1024]{3,2,0,1:T(8,128)(2,1)S(1)}, u32[]{:S(2)}, u32[]{:S(2)}) %all-to-all-start.1) | async-done | bytes 1048608 | tf_op jit(solution)/shard_map/all_to_all | solution.py:64
  68.8 0.1 copy.39
  69.0 0.9 while.36
  69.0 0.4 fusion.41
  69.4 0.4 fusion.41
  69.8 0.1 fusion.31
  70.0 0.7 collective-permute-start
  70.7 2.0 %collective-permute-start.1 = (f32[2,1,16]{2,0,1:T(2,128)S(1)}, f32[2,1,16]{2,0,1:T(2,128)S(1)}, u32[]{:S(2)}, u32[]{:S(2)}) collective-permute-start(f32[2,1,16]{2,0,1:T(2,128)S(1)} %get-tuple-element.159), channel_id=1, source_target_pairs={{0,2},{1,3},{2,0},{3,1},{4,6},{5,7},{6,4},{7,5},{8,10},{9,11},{10,... | collective-permute-start | bytes 392 | tf_op jit(solution)/shard_map/ppermute | solution.py:78
  72.7 2.8 %collective-permute-start.3 = (f32[2,1,16]{2,0,1:T(2,128)S(1)}, f32[2,1,16]{2,0,1:T(2,128)S(1)}, u32[]{:S(2)}, u32[]{:S(2)}) collective-permute-start(f32[2,1,16]{2,0,1:T(2,128)S(1)} %get-tuple-element.157), channel_id=1, source_target_pairs={{0,4},{1,5},{2,6},{3,7},{4,0},{5,1},{6,2},{7,3},{8,12},{9,13},{10,... | collective-permute-start | bytes 392 | tf_op jit(solution)/shard_map/ppermute | solution.py:78
  75.5 0.3 collective-permute-start.4
  75.9 2.6 %collective-permute-start.5 = (f32[2,1,16]{2,0,1:T(2,128)S(1)}, f32[2,1,16]{2,0,1:T(2,128)S(1)}, u32[]{:S(2)}, u32[]{:S(2)}) collective-permute-start(f32[2,1,16]{2,0,1:T(2,128)S(1)} %get-tuple-element.155), channel_id=1, source_target_pairs={{0,6},{1,7},{2,4},{3,5},{4,2},{5,3},{6,0},{7,1},{8,14},{9,15},{10,... | collective-permute-start | bytes 392 | tf_op jit(solution)/shard_map/ppermute | solution.py:78
  78.5 0.1 collective-permute-start.6
  78.7 2.9 %collective-permute-start.7 = (f32[2,1,16]{2,0,1:T(2,128)S(1)}, f32[2,1,16]{2,0,1:T(2,128)S(1)}, u32[]{:S(2)}, u32[]{:S(2)}) collective-permute-start(f32[2,1,16]{2,0,1:T(2,128)S(1)} %get-tuple-element.153), channel_id=1, source_target_pairs={{0,8},{1,9},{2,10},{3,11},{4,12},{5,13},{6,14},{7,15},{8,0},{9,1},... | collective-permute-start | bytes 392 | tf_op jit(solution)/shard_map/ppermute | solution.py:78
  81.6 0.1 collective-permute-start.8
  81.8 2.2 %collective-permute-start.9 = (f32[2,1,16]{2,0,1:T(2,128)S(1)}, f32[2,1,16]{2,0,1:T(2,128)S(1)}, u32[]{:S(2)}, u32[]{:S(2)}) collective-permute-start(f32[2,1,16]{2,0,1:T(2,128)S(1)} %get-tuple-element.151), channel_id=1, source_target_pairs={{0,10},{1,11},{2,8},{3,9},{4,14},{5,15},{6,12},{7,13},{8,2},{9,3},... | collective-permute-start | bytes 392 | tf_op jit(solution)/shard_map/ppermute | solution.py:78
  83.9 1.3 %collective-permute-start.10 = (f32[2,1,16]{2,0,1:T(2,128)S(1)}, f32[2,1,16]{2,0,1:T(2,128)S(1)}, u32[]{:S(2)}, u32[]{:S(2)}) collective-permute-start(f32[2,1,16]{2,0,1:T(2,128)S(1)} %get-tuple-element.150), channel_id=1, source_target_pairs={{0,11},{1,10},{2,9},{3,8},{4,15},{5,14},{6,13},{7,12},{8,3},{9,2},... | collective-permute-start | bytes 392 | tf_op jit(solution)/shard_map/ppermute | solution.py:78
  85.2 2.4 %collective-permute-start.11 = (f32[2,1,16]{2,0,1:T(2,128)S(1)}, f32[2,1,16]{2,0,1:T(2,128)S(1)}, u32[]{:S(2)}, u32[]{:S(2)}) collective-permute-start(f32[2,1,16]{2,0,1:T(2,128)S(1)} %get-tuple-element.149), channel_id=1, source_target_pairs={{0,12},{1,13},{2,14},{3,15},{4,8},{5,9},{6,10},{7,11},{8,4},{9,5},... | collective-permute-start | bytes 392 | tf_op jit(solution)/shard_map/ppermute | solution.py:78
  87.6 1.6 %collective-permute-start.12 = (f32[2,1,16]{2,0,1:T(2,128)S(1)}, f32[2,1,16]{2,0,1:T(2,128)S(1)}, u32[]{:S(2)}, u32[]{:S(2)}) collective-permute-start(f32[2,1,16]{2,0,1:T(2,128)S(1)} %get-tuple-element.148), channel_id=1, source_target_pairs={{0,13},{1,12},{2,15},{3,14},{4,9},{5,8},{6,11},{7,10},{8,5},{9,4},... | collective-permute-start | bytes 392 | tf_op jit(solution)/shard_map/ppermute | solution.py:78
  89.2 3.3 %collective-permute-start.13 = (f32[2,1,16]{2,0,1:T(2,128)S(1)}, f32[2,1,16]{2,0,1:T(2,128)S(1)}, u32[]{:S(2)}, u32[]{:S(2)}) collective-permute-start(f32[2,1,16]{2,0,1:T(2,128)S(1)} %get-tuple-element.147), channel_id=1, source_target_pairs={{0,14},{1,15},{2,12},{3,13},{4,10},{5,11},{6,8},{7,9},{8,6},{9,7},... | collective-permute-start | bytes 392 | tf_op jit(solution)/shard_map/ppermute | solution.py:78
  92.5 1.0 %collective-permute-start.14 = (f32[2,1,16]{2,0,1:T(2,128)S(1)}, f32[2,1,16]{2,0,1:T(2,128)S(1)}, u32[]{:S(2)}, u32[]{:S(2)}) collective-permute-start(f32[2,1,16]{2,0,1:T(2,128)S(1)} %get-tuple-element.146), channel_id=1, source_target_pairs={{0,15},{1,14},{2,13},{3,12},{4,11},{5,10},{6,9},{7,8},{8,7},{9,6},... | collective-permute-start | bytes 392 | tf_op jit(solution)/shard_map/ppermute | solution.py:78
  93.7 1.8 %collective-permute-done.13 = f32[2,1,16]{2,0,1:T(2,128)S(1)} collective-permute-done((f32[2,1,16]{2,0,1:T(2,128)S(1)}, f32[2,1,16]{2,0,1:T(2,128)S(1)}, u32[]{:S(2)}, u32[]{:S(2)}) %collective-permute-start.13) | collective-permute-done | bytes 160 | tf_op jit(solution)/shard_map/ppermute | solution.py:78
  95.6 2.7 %collective-permute-done.14 = f32[2,1,16]{2,0,1:T(2,128)S(1)} collective-permute-done((f32[2,1,16]{2,0,1:T(2,128)S(1)}, f32[2,1,16]{2,0,1:T(2,128)S(1)}, u32[]{:S(2)}, u32[]{:S(2)}) %collective-permute-start.14) | collective-permute-done | bytes 160 | tf_op jit(solution)/shard_map/ppermute | solution.py:78
  98.3 0.1 reshape.59
  98.4 2.5 %gather_fusion.2 = f32[256]{0:T(256)} fusion(f32[512]{0:T(512)S(1)} %reshape.59, s32[1024]{0:T(1024)S(1)} %pad_clamp_fusion.1), kind=kCustom, calls=%fused_computation.2 | custom fusion | bytes 3072 | tf_op jit(solution)/shard_map/gather | solution.py:81
  (97 shorter events, 1.0 us)
Async XLA Ops:
  0.0 0.7 copy-start
  5.8 30.1 %copy-start.1 = (bf16[256,1024]{1,0:T(8,128)(2,1)S(1)}, bf16[256,1024]{1,0:T(8,128)(2,1)}, u32[]{:S(2)}) copy-start(bf16[256,1024]{1,0:T(8,128)(2,1)} %param.6) | copy-start | bytes 1572868
  28.5 13.8 %all-to-all-start = ((bf16[2,16,16]{2,0,1:T(2,128)(2,1)}), bf16[2,16,16]{2,0,1:T(2,128)(2,1)S(1)}, u32[]{:S(2)}, u32[]{:S(2)}) async-start(bf16[2,16,16]{2,0,1:T(2,128)(2,1)} %copy.36), calls=%async_computation | async-start | bytes 16384 | tf_op jit(solution)/shard_map/all_to_all | solution.py:65
  42.3 26.5 %all-to-all-start.1 = ((bf16[2,16,16,1024]{3,2,0,1:T(8,128)(2,1)}), bf16[2,16,16,1024]{3,2,0,1:T(8,128)(2,1)S(1)}, u32[]{:S(2)}, u32[]{:S(2)}) async-start(bf16[2,16,16,1024]{3,2,0,1:T(8,128)(2,1)} %copy.38), calls=%async_computation.1 | async-start | bytes 2097152 | tf_op jit(solution)/shard_map/all_to_all | solution.py:64
  70.0 5.9 %collective-permute-start = (f32[2,1,16]{2,0,1:T(2,128)S(1)}, f32[2,1,16]{2,0,1:T(2,128)S(1)}, u32[]{:S(2)}, u32[]{:S(2)}) collective-permute-start(f32[2,1,16]{2,0,1:T(2,128)S(1)} %get-tuple-element.160), channel_id=1, source_target_pairs={{0,1},{1,0},{2,3},{3,2},{4,5},{5,4},{6,7},{7,6},{8,9},{9,8},{10,11... | collective-permute-start | bytes 392 | tf_op jit(solution)/shard_map/ppermute | solution.py:78
  70.7 7.8 %collective-permute-start.1 = (f32[2,1,16]{2,0,1:T(2,128)S(1)}, f32[2,1,16]{2,0,1:T(2,128)S(1)}, u32[]{:S(2)}, u32[]{:S(2)}) collective-permute-start(f32[2,1,16]{2,0,1:T(2,128)S(1)} %get-tuple-element.159), channel_id=1, source_target_pairs={{0,2},{1,3},{2,0},{3,1},{4,6},{5,7},{6,4},{7,5},{8,10},{9,11},{10,... | collective-permute-start | bytes 392 | tf_op jit(solution)/shard_map/ppermute | solution.py:78
  72.7 6.0 %collective-permute-start.2 = (f32[2,1,16]{2,0,1:T(2,128)S(1)}, f32[2,1,16]{2,0,1:T(2,128)S(1)}, u32[]{:S(2)}, u32[]{:S(2)}) collective-permute-start(f32[2,1,16]{2,0,1:T(2,128)S(1)} %get-tuple-element.158), channel_id=1, source_target_pairs={{0,3},{1,2},{2,1},{3,0},{4,7},{5,6},{6,5},{7,4},{8,11},{9,10},{10,... | collective-permute-start | bytes 392 | tf_op jit(solution)/shard_map/ppermute | solution.py:78
  72.7 8.9 %collective-permute-start.3 = (f32[2,1,16]{2,0,1:T(2,128)S(1)}, f32[2,1,16]{2,0,1:T(2,128)S(1)}, u32[]{:S(2)}, u32[]{:S(2)}) collective-permute-start(f32[2,1,16]{2,0,1:T(2,128)S(1)} %get-tuple-element.157), channel_id=1, source_target_pairs={{0,4},{1,5},{2,6},{3,7},{4,0},{5,1},{6,2},{7,3},{8,12},{9,13},{10,... | collective-permute-start | bytes 392 | tf_op jit(solution)/shard_map/ppermute | solution.py:78
  75.5 6.2 %collective-permute-start.4 = (f32[2,1,16]{2,0,1:T(2,128)S(1)}, f32[2,1,16]{2,0,1:T(2,128)S(1)}, u32[]{:S(2)}, u32[]{:S(2)}) collective-permute-start(f32[2,1,16]{2,0,1:T(2,128)S(1)} %get-tuple-element.156), channel_id=1, source_target_pairs={{0,5},{1,4},{2,7},{3,6},{4,1},{5,0},{6,3},{7,2},{8,13},{9,12},{10,... | collective-permute-start | bytes 392 | tf_op jit(solution)/shard_map/ppermute | solution.py:78
  75.9 8.1 %collective-permute-start.5 = (f32[2,1,16]{2,0,1:T(2,128)S(1)}, f32[2,1,16]{2,0,1:T(2,128)S(1)}, u32[]{:S(2)}, u32[]{:S(2)}) collective-permute-start(f32[2,1,16]{2,0,1:T(2,128)S(1)} %get-tuple-element.155), channel_id=1, source_target_pairs={{0,6},{1,7},{2,4},{3,5},{4,2},{5,3},{6,0},{7,1},{8,14},{9,15},{10,... | collective-permute-start | bytes 392 | tf_op jit(solution)/shard_map/ppermute | solution.py:78
  78.5 6.7 %collective-permute-start.6 = (f32[2,1,16]{2,0,1:T(2,128)S(1)}, f32[2,1,16]{2,0,1:T(2,128)S(1)}, u32[]{:S(2)}, u32[]{:S(2)}) collective-permute-start(f32[2,1,16]{2,0,1:T(2,128)S(1)} %get-tuple-element.154), channel_id=1, source_target_pairs={{0,7},{1,6},{2,5},{3,4},{4,3},{5,2},{6,1},{7,0},{8,15},{9,14},{10,... | collective-permute-start | bytes 392 | tf_op jit(solution)/shard_map/ppermute | solution.py:78
  78.7 9.0 %collective-permute-start.7 = (f32[2,1,16]{2,0,1:T(2,128)S(1)}, f32[2,1,16]{2,0,1:T(2,128)S(1)}, u32[]{:S(2)}, u32[]{:S(2)}) collective-permute-start(f32[2,1,16]{2,0,1:T(2,128)S(1)} %get-tuple-element.153), channel_id=1, source_target_pairs={{0,8},{1,9},{2,10},{3,11},{4,12},{5,13},{6,14},{7,15},{8,0},{9,1},... | collective-permute-start | bytes 392 | tf_op jit(solution)/shard_map/ppermute | solution.py:78
  81.6 7.6 %collective-permute-start.8 = (f32[2,1,16]{2,0,1:T(2,128)S(1)}, f32[2,1,16]{2,0,1:T(2,128)S(1)}, u32[]{:S(2)}, u32[]{:S(2)}) collective-permute-start(f32[2,1,16]{2,0,1:T(2,128)S(1)} %get-tuple-element.152), channel_id=1, source_target_pairs={{0,9},{1,8},{2,11},{3,10},{4,13},{5,12},{6,15},{7,14},{8,1},{9,0},... | collective-permute-start | bytes 392 | tf_op jit(solution)/shard_map/ppermute | solution.py:78
  81.8 10.7 %collective-permute-start.9 = (f32[2,1,16]{2,0,1:T(2,128)S(1)}, f32[2,1,16]{2,0,1:T(2,128)S(1)}, u32[]{:S(2)}, u32[]{:S(2)}) collective-permute-start(f32[2,1,16]{2,0,1:T(2,128)S(1)} %get-tuple-element.151), channel_id=1, source_target_pairs={{0,10},{1,11},{2,8},{3,9},{4,14},{5,15},{6,12},{7,13},{8,2},{9,3},... | collective-permute-start | bytes 392 | tf_op jit(solution)/shard_map/ppermute | solution.py:78
  83.9 9.6 %collective-permute-start.10 = (f32[2,1,16]{2,0,1:T(2,128)S(1)}, f32[2,1,16]{2,0,1:T(2,128)S(1)}, u32[]{:S(2)}, u32[]{:S(2)}) collective-permute-start(f32[2,1,16]{2,0,1:T(2,128)S(1)} %get-tuple-element.150), channel_id=1, source_target_pairs={{0,11},{1,10},{2,9},{3,8},{4,15},{5,14},{6,13},{7,12},{8,3},{9,2},... | collective-permute-start | bytes 392 | tf_op jit(solution)/shard_map/ppermute | solution.py:78
  85.2 8.4 %collective-permute-start.11 = (f32[2,1,16]{2,0,1:T(2,128)S(1)}, f32[2,1,16]{2,0,1:T(2,128)S(1)}, u32[]{:S(2)}, u32[]{:S(2)}) collective-permute-start(f32[2,1,16]{2,0,1:T(2,128)S(1)} %get-tuple-element.149), channel_id=1, source_target_pairs={{0,12},{1,13},{2,14},{3,15},{4,8},{5,9},{6,10},{7,11},{8,4},{9,5},... | collective-permute-start | bytes 392 | tf_op jit(solution)/shard_map/ppermute | solution.py:78
  87.6 6.0 %collective-permute-start.12 = (f32[2,1,16]{2,0,1:T(2,128)S(1)}, f32[2,1,16]{2,0,1:T(2,128)S(1)}, u32[]{:S(2)}, u32[]{:S(2)}) collective-permute-start(f32[2,1,16]{2,0,1:T(2,128)S(1)} %get-tuple-element.148), channel_id=1, source_target_pairs={{0,13},{1,12},{2,15},{3,14},{4,9},{5,8},{6,11},{7,10},{8,5},{9,4},... | collective-permute-start | bytes 392 | tf_op jit(solution)/shard_map/ppermute | solution.py:78
  89.2 6.3 %collective-permute-start.13 = (f32[2,1,16]{2,0,1:T(2,128)S(1)}, f32[2,1,16]{2,0,1:T(2,128)S(1)}, u32[]{:S(2)}, u32[]{:S(2)}) collective-permute-start(f32[2,1,16]{2,0,1:T(2,128)S(1)} %get-tuple-element.147), channel_id=1, source_target_pairs={{0,14},{1,15},{2,12},{3,13},{4,10},{5,11},{6,8},{7,9},{8,6},{9,7},... | collective-permute-start | bytes 392 | tf_op jit(solution)/shard_map/ppermute | solution.py:78
  92.5 5.8 %collective-permute-start.14 = (f32[2,1,16]{2,0,1:T(2,128)S(1)}, f32[2,1,16]{2,0,1:T(2,128)S(1)}, u32[]{:S(2)}, u32[]{:S(2)}) collective-permute-start(f32[2,1,16]{2,0,1:T(2,128)S(1)} %get-tuple-element.146), channel_id=1, source_target_pairs={{0,15},{1,14},{2,13},{3,12},{4,11},{5,10},{6,9},{7,8},{8,7},{9,6},... | collective-permute-start | bytes 392 | tf_op jit(solution)/shard_map/ppermute | solution.py:78
